TPU v7x, 8 devices: a whole 2x2x1 slice. The times are simulated.
8 devices in a mesh: data: 1 (over z), ffn: 2 (over y), hid: 4 (over x, core).
Axes of the slice: x: 2, y: 2, z: 1, core: 2. Of those that a mesh axis runs over, the one named last changes fastest.
Arguments:
- residual: bfloat16 [64, 4096], P('data', 'hid')
- gain_mlp: float32 [4096], P('hid')
- gain_attn: float32 [4096], P('hid')
- w_gate: bfloat16 [4096, 11008], P('hid', 'ffn')
- w_up: bfloat16 [4096, 11008], P('hid', 'ffn')
- w_down: bfloat16 [11008, 4096], P('ffn', 'hid')
- w_qkv: bfloat16 [4096, 12288], P('hid', 'ffn')
Outputs:
- output 1: bfloat16 [64, 4096], P('data', 'hid')
- output 2: bfloat16 [64, 12288], P('data', 'ffn')
All inputs are finite; a program needn't handle non-finite values.
Results may differ from a plain program's by a relative error of at most 0.0185647.
Values are sent between devices in bfloat16 or wider.
A program may use at most 1 GiB of HBM per device.

v0:
```python
import jax
import jax.numpy as jnp
from jax import lax
from jax.sharding import PartitionSpec as P

NORM_EPS = 1e-6


def solution(mesh):
    hid_ways = mesh.shape['hid']

    def shard_norm(resid_shard, gain_shard, d_model):
        resid32 = resid_shard.astype(jnp.float32)
        part_sq = jnp.sum(resid32 * resid32, axis=1, keepdims=True)
        full_sq = lax.psum(part_sq, 'hid')
        scale = lax.rsqrt(full_sq / d_model + NORM_EPS)
        return (resid32 * scale * gain_shard[None, :]).astype(jnp.bfloat16)

    def device_step(residual, gain_mlp, gain_attn, w_gate, w_up, w_down, w_qkv):
        d_model = residual.shape[1] * hid_ways
        normed = shard_norm(residual, gain_mlp, d_model)
        gate_part = jnp.dot(normed, w_gate, preferred_element_type=jnp.float32).astype(jnp.bfloat16)
        up_part = jnp.dot(normed, w_up, preferred_element_type=jnp.float32).astype(jnp.bfloat16)
        gate_sum, up_sum = lax.psum((gate_part, up_part), 'hid')
        hidden_act = (jax.nn.silu(gate_sum.astype(jnp.float32)) * up_sum.astype(jnp.float32)).astype(jnp.bfloat16)
        down_part = jnp.dot(hidden_act, w_down, preferred_element_type=jnp.float32).astype(jnp.bfloat16)
        down_sum = lax.psum(down_part, 'ffn')
        residual_out = (residual.astype(jnp.float32) + down_sum.astype(jnp.float32)).astype(jnp.bfloat16)
        normed_next = shard_norm(residual_out, gain_attn, d_model)
        qkv_part = jnp.dot(normed_next, w_qkv, preferred_element_type=jnp.float32).astype(jnp.bfloat16)
        qkv_out = lax.psum(qkv_part, 'hid')
        return residual_out, qkv_out

    return jax.shard_map(
        device_step, mesh=mesh,
        in_specs=(P('data', 'hid'), P('hid'), P('hid'), P('hid', 'ffn'), P('hid', 'ffn'),
                  P('ffn', 'hid'), P('hid', 'ffn')),
        out_specs=(P('data', 'hid'), P('data', 'ffn')),
        check_vma=False)
```

profile of v0, /device:TPU:0, one launch (start us, length us, event | category | flops | bytes accessed | tf_op | source)
XLA Modules:
  0.0 139.2 jit_solution(10649727915487389852)
XLA Ops:
  7.2 0.0 copy-start.1
  7.2 0.0 copy-start.3
  7.2 0.0 all-reduce.9.cloned.1.call-start
  7.2 1.0 fusion.10
  8.3 8.8 %psum.42 = f32[64,1]{0,1:T(1,128)S(1)} all-reduce(f32[64,1]{0,1:T(1,128)S(1)} %bitcast.11), channel_id=1, replica_groups=mesh['data'=1,'ffn'=2,'hid'=4] {'hid'}, use_global_device_ids=true, to_apply=%region_1.0 | all-reduce | flops 64 | bytes 512 | tf_op jit(solution)/shard_map/psum | solution.py:15
  17.0 0.0 copy-start
  17.0 7.4 %convolution_convert_fusion.1 = bf16[64,5504]{1,0:T(8,128)(2,1)} fusion(bf16[1024,5504]{1,0:T(8,128)(2,1)} %param.11, bf16[64,1024]{1,0:T(8,128)(2,1)} %param.7, f32[1024]{0:T(1024)} %param.8, f32[64]{0:T(128)S(1)} %rsqrt_bitcast_fusion.1), kind=kOutput, calls=%fused_computation.1 | convolution fusion | flops 722034688 | bytes 12112128 | tf_op jit(solution)/shard_map/dot_general | solution.py:23
  24.5 0.0 copy-done.1
  24.5 0.0 copy-done.3
  24.5 0.1 copy-done
  24.5 3.0 %convolution_convert_fusion.2 = bf16[64,5504]{1,0:T(8,128)(2,1)} fusion(bf16[1024,5504]{1,0:T(8,128)(2,1)S(1)} %copy-done, bf16[64,1024]{1,0:T(8,128)(2,1)S(1)} %copy-done.1, f32[1024]{0:T(1024)S(1)} %copy-done.3, f32[64]{0:T(128)S(1)} %rsqrt_bitcast_fusion.1), kind=kOutput, calls=%fused_computation.2 | convolution fusion | flops 722034688 | bytes 12112128 | tf_op jit(solution)/shard_map/dot_general | solution.py:22
  27.5 0.0 all-reduce.9.cloned.1.call-update
  27.6 0.0 all-reduce.5.cloned.1.call-start
  27.6 35.2 %all-reduce.9.cloned.1.call-done = (bf16[64,5504]{1,0:T(8,128)(2,1)}, bf16[64,5504]{1,0:T(8,128)(2,1)}) async-done(((bf16[64,5504]{1,0:T(8,128)(2,1)}, bf16[64,5504]{1,0:T(8,128)(2,1)}), (bf16[64,5504]{1,0:T(8,128)(2,1)}, bf16[64,5504]{1,0:T(8,128)(2,1)})) %all-reduce.9.cloned.1.call-update) | async-done | bytes 1409040 | tf_op jit(solution)/shard_map/psum | solution.py:24
  62.8 0.0 copy-start.4
  62.8 7.4 %convolution_convert_fusion.3 = bf16[64,1024]{1,0:T(8,128)(2,1)} fusion(bf16[5504,1024]{1,0:T(8,128)(2,1)} %param.12, bf16[64,5504]{1,0:T(8,128)(2,1)} %get-tuple-element.2, bf16[64,5504]{1,0:T(8,128)(2,1)} %get-tuple-element.3), kind=kOutput, calls=%fused_computation.10 | convolution fusion | flops 724303872 | bytes 12812288 | tf_op jit(solution)/shard_map/dot_general | solution.py:26
  70.2 0.0 all-reduce.5.cloned.1.call-update
  70.3 0.0 all-reduce.7.cloned.1.call-start
  70.3 15.9 %all-reduce.5.cloned.1.call-done = bf16[64,1024]{1,0:T(8,128)(2,1)} async-done(((bf16[64,1024]{1,0:T(8,128)(2,1)}), bf16[64,1024]{1,0:T(8,128)(2,1)}) %all-reduce.5.cloned.1.call-update) | async-done | bytes 131088 | tf_op jit(solution)/shard_map/psum | solution.py:27
  86.2 1.1 fusion.7
  87.3 0.0 copy-start.2
  87.3 6.1 %psum.46 = f32[64,1]{0,1:T(1,128)S(1)} all-reduce(f32[64,1]{0,1:T(1,128)S(1)} %bitcast.10), channel_id=1, replica_groups=mesh['data'=1,'ffn'=2,'hid'=4] {'hid'}, use_global_device_ids=true, to_apply=%region_6.7 | all-reduce | flops 64 | bytes 512 | tf_op jit(solution)/shard_map/psum | solution.py:15
  93.4 0.0 copy-done.4
  93.4 7.8 %convolution_convert_fusion = bf16[64,6144]{1,0:T(8,128)(2,1)} fusion(bf16[1024,6144]{1,0:T(8,128)(2,1)} %param.13, bf16[64,1024]{1,0:T(8,128)(2,1)S(1)} %get-tuple-element.6, f32[1024]{0:T(1024)S(1)} %copy-done.4, f32[64]{0:T(128)S(1)} %rsqrt_bitcast_fusion), kind=kOutput, calls=%fused_computation | convolution fusion | flops 805961728 | bytes 13504768 | tf_op jit(solution)/shard_map/dot_general | solution.py:30
  101.2 0.0 all-reduce.7.cloned.1.call-update
  101.2 29.4 %all-reduce.7.cloned.1.call-done = bf16[64,6144]{1,0:T(8,128)(2,1)} async-done(((bf16[64,6144]{1,0:T(8,128)(2,1)}), bf16[64,6144]{1,0:T(8,128)(2,1)}) %all-reduce.7.cloned.1.call-update) | async-done | bytes 786448 | tf_op jit(solution)/shard_map/psum | solution.py:31
  130.6 2.1 %copy.13 = bf16[64,6144]{1,0:T(8,128)(2,1)} copy(bf16[64,6144]{1,0:T(8,128)(2,1)} %all-reduce.7.cloned.1.call-done) | data formatting | bytes 1572864
  132.7 0.0 copy-done.2
  (2 shorter events, 0.0 us)
Async XLA Ops:
  7.2 17.3 %copy-start.1 = (bf16[64,1024]{1,0:T(8,128)(2,1)S(1)}, bf16[64,1024]{1,0:T(8,128)(2,1)}, u32[]{:S(2)}) copy-start(bf16[64,1024]{1,0:T(8,128)(2,1)} %param.7) | copy-start | bytes 393220
  7.2 17.3 %copy-start.3 = (f32[1024]{0:T(1024)S(1)}, f32[1024]{0:T(1024)}, u32[]{:S(2)}) copy-start(f32[1024]{0:T(1024)} %param.8) | copy-start | bytes 12292
  7.2 55.7 %all-reduce.9.cloned.1.call-start = ((), (), s32[]{:S(2)}) async-start(), calls=%async_computation.2 | async-start | bytes 2818048 | tf_op jit(solution)/shard_map/psum | solution.py:24
  17.0 7.5 %copy-start = (bf16[1024,5504]{1,0:T(8,128)(2,1)S(1)}, bf16[1024,5504]{1,0:T(8,128)(2,1)}, u32[]{:S(2)}) copy-start(bf16[1024,5504]{1,0:T(8,128)(2,1)} %param.10) | copy-start | bytes 33816580
  27.6 58.6 %all-reduce.5.cloned.1.call-start = ((), (), s32[]{:S(2)}) async-start(), calls=%async_computation | async-start | bytes 262144 | tf_op jit(solution)/shard_map/psum | solution.py:27
  62.8 30.5 %copy-start.4 = (f32[1024]{0:T(1024)S(1)}, f32[1024]{0:T(1024)}, u32[]{:S(2)}) copy-start(f32[1024]{0:T(1024)} %param.9) | copy-start | bytes 12292
  70.3 60.4 %all-reduce.7.cloned.1.call-start = ((), (), s32[]{:S(2)}) async-start(), calls=%async_computation.1 | async-start | bytes 1572864 | tf_op jit(solution)/shard_map/psum | solution.py:31
  87.3 45.4 %copy-start.2 = (bf16[64,1024]{1,0:T(8,128)(2,1)}, bf16[64,1024]{1,0:T(8,128)(2,1)S(1)}, u32[]{:S(2)}) copy-start(bf16[64,1024]{1,0:T(8,128)(2,1)S(1)} %get-tuple-element.6) | copy-start | bytes 393220
Sparse Core Ops, SparseCore 0:
  27.7 35.1 all-reduce.8
  70.4 15.7 all-reduce.4
  101.4 29.2 all-reduce.6
where the time goes:
time: 139 us
  waiting for transfers between devices  80.6 us (58%)
  matrix products  25.7 us (18%)
  blocking collectives  14.9 us (11%)
  between operations  13.8 us (10%)
  local copies, waits for them, and re-layouts  2.14 us (2%)
  other arithmetic  2.11 us (2%)
    psum x1, waiting for transfers between devices, device_step(): gate_sum, up_sum = lax.psum((gate_part, up_part), 'hid')  35.2 us
    psum x1, waiting for transfers between devices, device_step(): qkv_out = lax.psum(qkv_part, 'hid')  29.4 us
    psum x1, waiting for transfers between devices, device_step(): down_sum = lax.psum(down_part, 'ffn')  15.9 us
    psum x2, blocking collectives, shard_norm(): full_sq = lax.psum(part_sq, 'hid')  14.9 us
    dot_general x1, matrix products, device_step(): jnp.dot(normed_next, w_qkv, preferred_element_type=jnp.float32)  7.83 us
    dot_general x1, matrix products, device_step(): jnp.dot(normed, w_up, preferred_element_type=jnp.float32)  7.42 us
    dot_general x1, matrix products, device_step(): jnp.dot(hidden_act, w_down, preferred_element_type=jnp.float32)  7.39 us
    dot_general x1, matrix products, device_step(): jnp.dot(normed, w_gate, preferred_element_type=jnp.float32)  3.02 us
  transfers between devices with their start and end apart: 3, of which 3 were waited for; matrix products, arithmetic and copies ran while one was open for 0% of the time, Pallas kernels for 0%

commit v1 on v0

v1 whole, which is shorter than its diff:
```python
import jax
import jax.numpy as jnp
from jax import lax
from jax.experimental import pallas as pl
from jax.experimental.pallas import tpu as pltpu
from jax.sharding import PartitionSpec as P

NORM_EPS = 1e-6
F32 = jnp.float32
BF16 = jnp.bfloat16
MESH = pl.DeviceIdType.MESH

ROWS = 64
DW = 1024
FF = 5504
QW = 6144
D_MODEL = 4096
G = 2
T = ROWS // G
H = T // 2
Q = T // 4
W = 512
NC = 11
LAST = FF - W
WQ = 1024
NQ = QW // WQ
AHEAD = 4


def kernel(x_hbm, g1_hbm, g2_hbm, wg_hbm, wu_hbm, wd_hbm, wq_hbm,
           x2_out, q_out,
           wg, wu, wd, wq, xv, g1, g2, nv, x2v, n2v,
           part, recv1, xsend, recv2, abuf, acc, dsend, drecv,
           ss_send, ss_recv, qpart, qrecv1, qx, qrecv2,
           s_in, s_wg, s_wu, s_wd, s_wq,
           d1s, d1r, rss, rsr, ags, agr, fws, fwr, ys, yr, sss, ssr,
           qds, qdr, qxs, qxr, qfs, qfr, s_x2):
    f = lax.axis_index('ffn')
    h = lax.axis_index('hid')
    xi, c = h // 2, h % 2
    mate = xi * 2 + (1 - c)
    across = (1 - xi) * 2 + c
    cross = (1 - xi) * 2 + (1 - c)
    pos = 2 * c + xi

    def rdma(src, dst, ssem, rsem, **dev):
        return pltpu.make_async_remote_copy(
            src_ref=src, dst_ref=dst, send_sem=ssem, recv_sem=rsem,
            device_id=dev, device_id_type=MESH)

    ld_x = pltpu.make_async_copy(x_hbm, xv, s_in.at[0])
    ld_g1 = pltpu.make_async_copy(g1_hbm, g1, s_in.at[1])
    ld_g2 = pltpu.make_async_copy(g2_hbm, g2, s_in.at[2])

    def col(i):
        return pl.multiple_of(jnp.minimum(i * W, LAST), 128)

    def ld_wg(i):
        return pltpu.make_async_copy(wg_hbm.at[:, pl.ds(col(i), W)], wg.at[i], s_wg.at[i])

    def ld_wu(i):
        return pltpu.make_async_copy(wu_hbm.at[:, pl.ds(col(i), W)], wu.at[i], s_wu.at[i])

    def ld_wd(i):
        return pltpu.make_async_copy(wd_hbm.at[pl.ds(col(i), W), :], wd.at[i], s_wd.at[i])

    def ld_wq(k):
        return pltpu.make_async_copy(
            wq_hbm.at[:, pl.ds(pl.multiple_of(k * WQ, WQ), WQ)], wq.at[k], s_wq.at[k])

    ld_x.start()
    ld_g1.start()

    @pl.loop(0, AHEAD)
    def _(i):
        ld_wg(i).start()
        ld_wu(i).start()

    ld_g2.start()

    barrier = pltpu.get_barrier_semaphore()
    for dev in ({'hid': mate}, {'hid': across}, {'hid': cross}, {'ffn': 1 - f}):
        pl.semaphore_signal(barrier, inc=1, device_id=dev, device_id_type=MESH)

    def ss_copies(e):
        return [rdma(ss_send.at[e], ss_recv.at[e, j], sss.at[e, j], ssr.at[e, j], hid=dev)
                for j, dev in enumerate((mate, across, cross))]

    def ss_put(e, rows32):
        n_rows = rows32.shape[0]
        row = jnp.sum(rows32 * rows32, axis=1, keepdims=True)
        eye = (lax.broadcasted_iota(jnp.int32, (n_rows, 128), 0)
               == lax.broadcasted_iota(jnp.int32, (n_rows, 128), 1))
        ss_send[e] = jnp.sum(jnp.where(eye, row, 0.0), axis=0, keepdims=True)

    def ss_get(e, n_rows):
        for cp in ss_copies(e):
            cp.wait_recv()
        tot = (ss_send[e] + ss_recv[e, 0]) + (ss_recv[e, 1] + ss_recv[e, 2])
        eye = (lax.broadcasted_iota(jnp.int32, (n_rows, 128), 0)
               == lax.broadcasted_iota(jnp.int32, (n_rows, 128), 1))
        full = jnp.sum(jnp.where(eye, tot, 0.0), axis=1, keepdims=True)
        return lax.rsqrt(full / D_MODEL + NORM_EPS)

    ld_x.wait()
    ss_put(0, xv[...].astype(F32))
    pl.semaphore_wait(barrier, 4)
    for cp in ss_copies(0):
        cp.start()
    ld_g1.wait()
    ld_g2.wait()
    scale = ss_get(0, ROWS)
    nv[...] = (xv[...].astype(F32) * scale * g1[...]).astype(BF16)

    def d1(i):
        return rdma(part.at[i, 1 - c], recv1.at[i], d1s.at[i], d1r.at[i], hid=mate)

    def rs(g, i):
        return rdma(xsend.at[g, i, 1 - xi], recv2.at[g, i], rss.at[g, i], rsr.at[g, i], hid=across)

    def ag(g, i):
        return rdma(abuf.at[g, i, pos], abuf.at[g, i, pos], ags.at[g, i], agr.at[g, i], hid=across)

    def fw(g, i):
        return rdma(abuf.at[g, i, pl.ds(2 * c, 2)], abuf.at[g, i, pl.ds(2 * c, 2)],
                    fws.at[g, i], fwr.at[g, i], hid=mate)

    def stage_gemm(i):
        @pl.when(i + AHEAD < NC)
        def _():
            ld_wg(i + AHEAD).start()
            ld_wu(i + AHEAD).start()

        @pl.when(i + AHEAD >= NC)
        def _():
            for j in range(3):
                k = (i + AHEAD - NC) * 3 + j

                @pl.when(k < NC)
                def _(k=k):
                    ld_wd(k).start()

        ld_wg(i).wait()
        ld_wu(i).wait()
        for u, w_ref in enumerate((wg, wu)):
            p = jnp.dot(nv[...], w_ref[i], preferred_element_type=F32).astype(BF16)
            for g in range(G):
                for half in range(2):
                    r = g * T + half * H
                    part[i, half, g, u] = p[r:r + H]
        d1(i).start()

    def stage_core_sum(i):
        d1(i).wait_recv()
        for g in range(G):
            s = [part[i, c, g, u].astype(F32) + recv1[i, g, u].astype(F32) for u in range(2)]
            for v in range(2):
                xsend[g, i, v] = jnp.concatenate(
                    [s[0][v * Q:(v + 1) * Q], s[1][v * Q:(v + 1) * Q]], axis=0).astype(BF16)

    def stage_act(g, i):
        rs(g, i).wait_recv()
        tot = (xsend[g, i, xi].astype(F32) + recv2[g, i].astype(F32)).astype(BF16).astype(F32)
        a = jax.nn.silu(tot[:Q]) * tot[Q:]
        lane = lax.broadcasted_iota(jnp.int32, (Q, W), 1)
        dup = jnp.where(i == NC - 1, NC * W - FF, 0)
        abuf[g, i, pos] = jnp.where(lane < dup, 0.0, a).astype(BF16)
        ag(g, i).start()

    def stage_forward(g, i):
        ag(g, i).wait_recv()
        fw(g, i).start()

    def stage_down(g, i):
        @pl.when(g == 0)
        def _():
            ld_wd(i).wait()

        fw(g, i).wait_recv()
        a = abuf[g, i].astype(F32).reshape(T, W).astype(BF16)
        acc[g] += jnp.dot(a, wd[i], preferred_element_type=F32)

    def yx(g):
        return rdma(dsend.at[g], drecv.at[g], ys.at[g], yr.at[g], ffn=1 - f)

    def down_send(g):
        dsend[g] = acc[g].astype(BF16)
        yx(g).start()

    def resid(g):
        yx(g).wait_recv()
        dn = (dsend[g].astype(F32) + drecv[g].astype(F32)).astype(BF16).astype(F32)
        x2 = (xv[g * T:(g + 1) * T].astype(F32) + dn).astype(BF16)
        x2v[g * T:(g + 1) * T] = x2
        ss_put(1 + g, x2.astype(F32))
        for cp in ss_copies(1 + g):
            cp.start()

    def norm2(g):
        s2 = ss_get(1 + g, T)
        n2v[g] = (x2v[g * T:(g + 1) * T].astype(F32) * s2 * g2[...]).astype(BF16)

    acc[...] = jnp.zeros_like(acc)

    LA, LB = 5, NC + 1
    SA = (LA, LA + 3, LA + 5)
    SB = (LB + 5, LB + 8, LB + 10)
    RES0 = SA[2] + NC + 6
    NRM0 = RES0 + 4
    END = SB[2] + NC

    def at(i, lag, fn):
        k = i - lag

        @pl.when(jnp.logical_and(k >= 0, k < NC))
        def _():
            fn(k)

    @pl.loop(0, END)
    def _(i):
        at(i, 0, stage_gemm)

        def sum_send(k):
            stage_core_sum(k)
            rs(0, k).start()
        at(i, 1, sum_send)
        at(i, LB, lambda k: rs(1, k).start())
        at(i, LB, lambda k: pl.when(k < NQ)(lambda: ld_wq(k).start()))
        at(i, SA[0], lambda k: stage_act(0, k))
        at(i, SA[1], lambda k: stage_forward(0, k))
        at(i, SA[2], lambda k: stage_down(0, k))
        pl.when(i == SA[2] + NC - 1)(lambda: down_send(0))
        at(i, SB[0], lambda k: stage_act(1, k))
        at(i, SB[1], lambda k: stage_forward(1, k))
        at(i, SB[2], lambda k: stage_down(1, k))
        pl.when(i == RES0)(lambda: resid(0))
        pl.when(i == NRM0)(lambda: norm2(0))

    down_send(1)

    def qd(g, k):
        return rdma(qpart.at[g, k, 1 - c], qrecv1.at[g, k], qds.at[g, k], qdr.at[g, k], hid=mate)

    def qe(g, k):
        return rdma(qx.at[g, k], qrecv2.at[g, k], qxs.at[g, k], qxr.at[g, k], hid=across)

    def qcols(k):
        return pl.ds(pl.multiple_of(k * WQ, WQ), WQ)

    def qf(g, k):
        ref = q_out.at[pl.ds(pl.multiple_of(g * T + c * H, H), H), qcols(k)]
        return rdma(ref, ref, qfs.at[g, k], qfr.at[g, k], hid=mate)

    def q_gemm(g, k):
        if g == 0:
            ld_wq(k).wait()
        p = jnp.dot(n2v[g], wq[k], preferred_element_type=F32).astype(BF16)
        for half in range(2):
            qpart[g, k, half] = p[half * H:(half + 1) * H]
        qd(g, k).start()

    def q_sum(g, k):
        qd(g, k).wait_recv()
        qx[g, k] = (qpart[g, k, c].astype(F32) + qrecv1[g, k].astype(F32)).astype(BF16)
        qe(g, k).start()

    def q_fin(g, k):
        qe(g, k).wait_recv()
        v = (qx[g, k].astype(F32) + qrecv2[g, k].astype(F32)).astype(BF16)
        q_out[pl.ds(pl.multiple_of(g * T + c * H, H), H), qcols(k)] = v
        qf(g, k).start()

    def q_push(g):
        @pl.loop(0, NQ + 1)
        def _(k):
            pl.when(k < NQ)(lambda: q_gemm(g, k))
            pl.when(k > 0)(lambda: q_sum(g, k - 1))

    q_push(0)
    resid(1)
    x2_out[...] = x2v[...]
    pl.loop(0, 2)(lambda k: q_fin(0, k))
    norm2(1)
    q_push(1)
    pl.loop(2, NQ)(lambda k: q_fin(0, k))
    pl.loop(0, NQ)(lambda k: q_fin(1, k))

    @pl.loop(0, NQ)
    def _(k):
        for g in range(G):
            qf(g, k).wait_recv()
            qf(g, k).wait_send()
            qd(g, k).wait_send()
            qe(g, k).wait_send()

    @pl.loop(0, NC)
    def _(i):
        d1(i).wait_send()
        for g in range(G):
            rs(g, i).wait_send()
            ag(g, i).wait_send()
            fw(g, i).wait_send()

    for g in range(G):
        yx(g).wait_send()
    for e in range(1 + G):
        for cp in ss_copies(e):
            cp.wait_send()


def solution(mesh):
    def device_step(residual, gain_mlp, gain_attn, w_gate, w_up, w_down, w_qkv):
        V = pltpu.VMEM
        D = pltpu.SemaphoreType.DMA
        scratch = [
            V((NC, DW, W), BF16), V((NC, DW, W), BF16), V((NC, W, DW), BF16), V((NQ, DW, WQ), BF16),
            V((ROWS, DW), BF16), V((1, DW), F32), V((1, DW), F32),
            V((ROWS, DW), BF16), V((ROWS, DW), BF16), V((G, T, DW), BF16),
            V((NC, 2, G, 2, H, W), BF16), V((NC, G, 2, H, W), BF16),
            V((G, NC, 2, 2 * Q, W), BF16), V((G, NC, 2 * Q, W), BF16),
            V((G, NC, 4, Q, W), BF16), V((G, T, DW), F32), V((G, T, DW), BF16), V((G, T, DW), BF16),
            V((1 + G, 1, 128), F32), V((1 + G, 3, 1, 128), F32),
            V((G, NQ, 2, H, WQ), BF16), V((G, NQ, H, WQ), BF16), V((G, NQ, H, WQ), BF16),
            V((G, NQ, H, WQ), BF16),
            D((3,)), D((NC,)), D((NC,)), D((NC,)), D((NQ,)),
            D((NC,)), D((NC,)),
            D((G, NC)), D((G, NC)), D((G, NC)), D((G, NC)), D((G, NC)), D((G, NC)),
            D((G,)), D((G,)), D((1 + G, 3)), D((1 + G, 3)),
            D((G, NQ)), D((G, NQ)), D((G, NQ)), D((G, NQ)), D((G, NQ)), D((G, NQ)), D((1,)),
        ]
        any_spec = pl.BlockSpec(memory_space=pl.ANY)
        vmem_spec = pl.BlockSpec(memory_space=pltpu.VMEM)
        return pl.pallas_call(
            kernel,
            out_shape=(jax.ShapeDtypeStruct((ROWS, DW), BF16), jax.ShapeDtypeStruct((ROWS, QW), BF16)),
            in_specs=[any_spec] * 7,
            out_specs=(vmem_spec, vmem_spec),
            scratch_shapes=scratch,
            compiler_params=pltpu.CompilerParams(
                collective_id=0, has_side_effects=True, vmem_limit_bytes=67_000_000),
        )(residual, gain_mlp[None, :], gain_attn[None, :], w_gate, w_up, w_down, w_qkv)

    return jax.shard_map(
        device_step, mesh=mesh,
        in_specs=(P('data', 'hid'), P('hid'), P('hid'), P('hid', 'ffn'), P('hid', 'ffn'),
                  P('ffn', 'hid'), P('hid', 'ffn')),
        out_specs=(P('data', 'hid'), P('data', 'ffn')),
        check_vma=False)
```

time: 139 us -> 57.4 us (0.41)
  waiting for transfers between devices: 80.6 us -> 0 us
  Pallas kernels: 0 us -> 53 us
  matrix products: 25.7 us -> 0 us
  blocking collectives: 14.9 us -> 0 us
  between operations: 13.8 us -> 0.64 us
  other arithmetic: 2.11 us -> 0 us
  local copies, waits for them, and re-layouts: 2.14 us -> 3.63 us
    psum x3 -> x0, waiting for transfers between devices: 80.5 us -> none  [the longest x1 35.2 us: device_step(): gate_sum, up_sum = lax.psum((gate_part, up_part), 'hid')]
    pallas_call x0 -> x1, Pallas kernels: none -> 53 us  [device_step(): pl.pallas_call(kernel, out_shape=(jax.ShapeDtypeStruct((ROWS, DW), BF16),...]
    dot_general x4 -> x0, matrix products: 25.7 us -> none  [the longest x1 7.83 us: device_step(): jnp.dot(normed_next, w_qkv, preferred_element_type=jnp.float32)]
    psum x2 -> x0, blocking collectives: 14.9 us -> none  [shard_norm(): full_sq = lax.psum(part_sq, 'hid')]
    reduce_sum x2 -> x0, other arithmetic: 2.09 us -> none  [shard_norm(): part_sq = jnp.sum(resid32 * resid32, axis=1, keepdims=True)]
    unnamed x11 -> x2, local copies, waits for them, and re-layouts: 2.14 us -> 3.63 us
  transfers between devices with their start and end apart: 3 -> 0, of which waited for: 3 -> 0; matrix products, arithmetic and copies ran while one was open for 0% -> 0% of each run, Pallas kernels for 0% -> 0%
where the time goes in v1:
time: 57.4 us; the launch traced here: 57.2 us
  Pallas kernels  53 us (92%)
  local copies, waits for them, and re-layouts  3.63 us (6%)
  between operations  0.64 us (1%)
    pallas_call x1, Pallas kernels, device_step(): pl.pallas_call(kernel, out_shape=(jax.ShapeDtypeStruct((ROWS, DW), BF16),...  53 us
    unnamed x2, local copies, waits for them, and re-layouts  3.63 us

profile of v1, /device:TPU:0, one launch (start us, length us, event | category | flops | bytes accessed | tf_op | source)
XLA Modules:
  0.0 57.2 jit_solution(4029201938270141492)
XLA Ops:
  0.6 53.0 %shard_map.86 = (bf16[64,1024]{1,0:T(8,128)(2,1)}, bf16[64,6144]{1,0:T(8,128)(2,1)}) custom-call(bf16[64,1024]{1,0:T(8,128)(2,1)} %x_hbm.1, f32[1,1024]{1,0:T(1,128)} %bitcast.2, f32[1,1024]{1,0:T(1,128)} %bitcast.3, bf16[1024,5504]{1,0:T(8,128)(2,1)} %wg_hbm.1, bf16[1024,5504]{1,0:T(8,128)(2,1)} %wu_hbm.1, bf16[5504,1024]{1,0:T(8,128)(2,1)} %wd_hbm.1, ...), custom_call_target="tpu_custom_call" | custom-call | tf_op jit(solution)/shard_map/pallas_call | solution.py:333
  53.6 1.6 %copy.11 = bf16[64,1024]{1,0:T(8,128)(2,1)} copy(bf16[64,1024]{1,0:T(8,128)(2,1)} %get-tuple-element.4) | data formatting | bytes 262144
  55.2 2.1 %copy.12 = bf16[64,6144]{1,0:T(8,128)(2,1)} copy(bf16[64,6144]{1,0:T(8,128)(2,1)} %get-tuple-element.5) | data formatting | bytes 1572864
